TPU v7x, 32 devices: a whole 2x2x4 slice. The times are simulated.
32 devices in a mesh: fsdp: 8 (over y, x, core), seq: 4 (over z).
Axes of the slice: x: 2, y: 2, z: 4, core: 2. Of those that a mesh axis runs over, the one named last changes fastest.
Arguments:
- layer_input: bfloat16 [8, 512, 4096], P('fsdp', 'seq'), may hold values from -6 to 6
- dt_weight: bfloat16 [4096, 64], P('fsdp'), may hold values from -0.09375 to 0.09375
- dt_bias: float32 [64], replicated, may hold values from -2 to -0.5
- decay_rate: float32 [64], replicated, may hold values from 0.0005 to 0.25
- ssm_input: bfloat16 [8, 512, 2048], P('fsdp', 'seq'), may hold values from -6 to 6
- in_basis: bfloat16 [8, 512, 512], P('fsdp', 'seq'), may hold values from -0.59765625 to 0.59765625
- out_basis: bfloat16 [8, 512, 512], P('fsdp', 'seq'), may hold values from -0.59765625 to 0.59765625
- out_cotangent: bfloat16 [8, 512, 2048], P('fsdp', 'seq'), may hold values from -6 to 6
Outputs:
- grad_input: bfloat16 [8, 512, 2048], P('fsdp', 'seq')
- grad_in_basis: bfloat16 [8, 512, 512], P('fsdp', 'seq')
- grad_out_basis: bfloat16 [8, 512, 512], P('fsdp', 'seq')
- grad_dt_weight: float32 [4096, 64], P('fsdp')
All inputs are finite; a program needn't handle non-finite values.
Results may differ from a plain program's by a relative error of at most 0.011.
Values may be sent and summed in bfloat16 or wider, within the bound.
A program may use at most 64 MiB of HBM per device.

v0:
```python
import jax
import jax.numpy as jnp
from jax import lax
from jax.sharding import PartitionSpec as P

STATE = 128
HIGH = lax.Precision.HIGHEST


def entering(value, axis, combine, identity):
    devices, position = (lax.axis_size(axis), lax.axis_index(axis))
    everything = jax.tree.map(
        lambda part, kind: lax.all_gather(part.astype(kind), axis),
        value,
        (jnp.bfloat16, jnp.bfloat16),
    )
    start = jax.tree.map(
        lambda part, zero: jnp.broadcast_to(jnp.asarray(zero, part.dtype), part.shape),
        value,
        identity,
    )

    def entering_step(k, before):
        reached = k < position
        new = combine(
            before, jax.tree.map(lambda part, own: part[k].astype(own.dtype), everything, value)
        )
        return jax.tree.map(lambda a, b: jnp.where(reached, a, b), new, before)

    return lax.fori_loop(0, devices, entering_step, start)


def prefix(value, axis, join, neutral):
    count, mine = (lax.axis_size(axis), lax.axis_index(axis))
    pieces = jax.tree.map(lambda part: lax.all_gather(part, axis), value)
    pieces = jax.tree.map(lambda part: part[::-1], pieces)
    mine = count - 1 - mine
    subtotal = jax.tree.map(
        lambda part, zero: jnp.full_like(part, 0) + jnp.asarray(zero, part.dtype), value, neutral
    )

    def prefix_step(position, subtotal):
        longer = join(subtotal, jax.tree.map(lambda part: part[position], pieces))
        return jax.tree.map(lambda new, old: jnp.where(position < mine, new, old), longer, subtotal)

    return lax.fori_loop(0, count - 1, prefix_step, subtotal)


def compose(earlier, later):
    decay_e, value_e = earlier
    decay_l, value_l = later
    return (decay_l * decay_e, value_l + decay_l[:, None, None] * value_e)


def body(
    layer_input, dt_weight, dt_bias, decay_rate, ssm_input, in_basis, out_basis, out_cotangent
):
    tokens = layer_input[0]
    length = tokens.shape[0]
    heads = dt_weight.shape[1]
    groups = in_basis.shape[2] // STATE
    per_group = heads // groups
    head_size = ssm_input.shape[2] // heads
    columns = tokens
    raw = (
        jnp.dot(
            columns,
            lax.all_gather(dt_weight, "fsdp", axis=0, tiled=True),
            preferred_element_type=jnp.float32,
        )
        + dt_bias
    )
    step_size = jax.nn.softplus(raw)
    rate_grid = decay_rate.reshape(groups, per_group)
    step_grid = step_size.reshape(length, groups, per_group)
    cumulative = jnp.cumsum(-decay_rate * step_size, axis=0).reshape(length, groups, per_group)
    final = cumulative[-1]
    tail = jnp.exp(final[None] - cumulative)
    leading = jnp.exp(cumulative)
    inputs_half = ssm_input[0].reshape(length, groups, per_group, head_size)
    upstream_half = out_cotangent[0].reshape(length, groups, per_group, head_size)
    bin_half = in_basis[0].reshape(length, groups, STATE)
    bout_half = out_basis[0].reshape(length, groups, STATE)
    inputs = inputs_half.astype(jnp.float32)
    upstream = upstream_half.astype(jnp.float32)
    basis_in = bin_half.astype(jnp.float32)
    basis_out = bout_half.astype(jnp.float32)
    position = jnp.arange(length)
    lower = position[:, None] >= position[None, :]
    cum_rows = cumulative.transpose(1, 2, 0)
    spread = cum_rows[:, :, :, None] - cum_rows[:, :, None, :]
    decay_mat = jnp.where(lower, jnp.exp(jnp.where(lower, spread, 0.0)), 0.0)
    intersection = jnp.einsum(
        "tgn,sgn->gts", bout_half, bin_half, preferred_element_type=jnp.float32
    )
    weighted = decay_mat * intersection[:, None]
    step_cols = step_grid.transpose(1, 2, 0)[:, :, None, :]
    local_state = jnp.einsum(
        "sgk,sgkp,sgn->gkpn", tail * step_grid, inputs, basis_in, precision=HIGH
    )
    local_grad = jnp.einsum("tgk,tgkp,tgn->gkpn", leading, upstream, basis_out, precision=HIGH)
    block_decay = jnp.exp(final).reshape(heads)
    flat_shape = (heads, head_size, STATE)
    grid_shape = (groups, per_group, head_size, STATE)
    identity = (jnp.ones((heads,), jnp.float32), jnp.zeros(flat_shape, jnp.float32))
    entry = entering((block_decay, local_state.reshape(flat_shape)), "seq", compose, identity)[
        1
    ].reshape(grid_shape)
    later = prefix((block_decay, local_grad.reshape(flat_shape)), "seq", compose, identity)[
        1
    ].reshape(grid_shape)
    pair = jnp.einsum(
        "tgkp,sgkp->gkts", upstream_half, inputs_half, preferred_element_type=jnp.float32
    )
    through = jnp.einsum("gkts,tgkp->sgkp", weighted, upstream, precision=HIGH)
    carried = jnp.einsum("sgn,gkpn->sgkp", basis_in, later, precision=HIGH)
    inner_x = through + tail[..., None] * carried
    grad_x = step_grid[..., None] * inner_x
    direct = jnp.sum(inputs * inner_x, axis=-1)
    scaled = decay_mat * pair * step_cols
    joint = jnp.sum(scaled, axis=1)
    moment = scaled * intersection[:, None]
    change = (jnp.sum(moment, axis=-1) - jnp.sum(moment, axis=-2)).transpose(2, 0, 1)
    grad_b = jnp.einsum("gts,tgn->sgn", joint, basis_out, precision=HIGH)
    grad_b = grad_b + jnp.einsum(
        "sgk,sgkp,gkpn->sgn", step_grid * tail, inputs, later, precision=HIGH
    )
    state_read = jnp.einsum("tgkp,gkpn->tgkn", upstream, entry, precision=HIGH)
    grad_c = jnp.einsum("gts,sgn->tgn", joint, basis_in, precision=HIGH)
    grad_c = grad_c + jnp.einsum("tgk,tgkn->tgn", leading, state_read, precision=HIGH)
    entry_term = leading * jnp.sum(state_read * basis_out[:, :, None, :], axis=-1)
    exit_term = tail * step_grid * jnp.sum(inputs * carried, axis=-1)
    closing = jnp.exp(final) * jnp.sum(later * entry, axis=(2, 3)) + jnp.sum(exit_term, axis=0)
    grad_cum = change + entry_term - exit_term
    grad_log = jnp.cumsum(grad_cum[::-1], axis=0)[::-1] + closing[None]
    grad_step = direct - rate_grid[None] * grad_log
    grad_raw = grad_step.reshape(length, heads) * jax.nn.sigmoid(raw)
    columns = tokens.astype(jnp.float32)
    partial_rows = lax.psum_scatter(
        jnp.dot(columns.T, grad_raw, precision=HIGH), "fsdp", scatter_dimension=0, tiled=True
    )
    grad_weight = lax.psum(partial_rows, "seq")
    out_x = grad_x.reshape(1, length, heads * head_size).astype(jnp.bfloat16)
    out_b = grad_b.reshape(1, length, groups * STATE).astype(jnp.bfloat16)
    out_c = grad_c.reshape(1, length, groups * STATE).astype(jnp.bfloat16)
    return (out_x, out_b, out_c, grad_weight)


def solution(mesh):
    placed = (
        P("fsdp", "seq", None),
        P("fsdp", None),
        P(),
        P(),
        P("fsdp", "seq", None),
        P("fsdp", "seq", None),
        P("fsdp", "seq", None),
        P("fsdp", "seq", None),
    )
    return jax.shard_map(
        body,
        mesh=mesh,
        in_specs=placed,
        out_specs=(
            P("fsdp", "seq", None),
            P("fsdp", "seq", None),
            P("fsdp", "seq", None),
            P("fsdp", None),
        ),
        check_vma=False,
    )
```

profile of v0, /device:TPU:0, one launch (start us, length us, event | category | flops | bytes accessed | tf_op | source)
XLA Modules:
  0.0 256.8 jit_solution(15940278393139724668)
XLA Ops:
  7.2 11.8 %all_gather.17 = bf16[4096,64]{0,1:T(8,128)(2,1)S(1)} all-gather(bf16[512,64]{0,1:T(8,128)(2,1)} %param.13), channel_id=1, replica_groups=mesh['fsdp'=8,'seq'=4] {'fsdp'}, dimensions={0}, use_global_device_ids=true | all-gather | bytes 589824 | tf_op jit(solution)/shard_map/all_gather | solution.py:68
  19.7 1.8 compare_select_fusion
  22.4 0.9 reshape_squeeze.13
  23.3 1.3 copy.82
  25.5 1.4 convolution_convert_fusion
  27.3 1.6 fusion.26
  30.1 11.6 %all-gather = f32[4,1,64]{2,1,0:T(1,128)S(1)} all-gather(f32[1,1,64]{2,1,0:T(1,128)} %get-tuple-element.277), channel_id=1, replica_groups=mesh['fsdp'=8,'seq'=4] {'seq'}, dimensions={0}, use_global_device_ids=true | all-gather | bytes 1280 | tf_op jit(solution)/shard_map/all_gather | solution.py:35
  42.4 8.4 %all-gather.1 = bf16[4,1,64]{2,1,0:T(2,128)(2,1)S(1)} all-gather(bf16[1,1,64]{2,1,0:T(2,128)(2,1)} %get-tuple-element.278), channel_id=1, replica_groups=mesh['fsdp'=8,'seq'=4] {'seq'}, dimensions={0}, use_global_device_ids=true | all-gather | bytes 640 | tf_op jit(solution)/shard_map/all_gather | solution.py:13
  53.1 5.1 %multiply_reduce_fusion = (f32[4,16,128]{2,1,0:T(8,128)}, f32[4,16,128]{2,1,0:T(8,128)}, f32[4,128,128]{2,1,0:T(8,128)}) fusion(f32[4,128,128]{2,1,0:T(8,128)S(1)} %fusion.40, f32[4,16,128]{2,1,0:T(8,128)} %bitcast.131, bf16[128,4,16,32]{0,3,2,1:T(8,128)(2,1)} %bitcast.120, bf16[128,4,16,32]{0,3,2,1:T(8,128)(2,1)} %bitcast.112, ...), kind=kOutput, calls=%fused_computation.15 | convolution fusion | flops 76464128 | bytes 1720320 | tf_op jit(solution)/shard_map/tgkp,sgkp->gkts/dot_general | solution.py:112
  58.2 14.8 %all-gather.7.cloned.1.call-done = bf16[4,64,32,128]{3,2,1,0:T(8,128)(2,1)} async-done(((bf16[1,64,32,128]{3,2,1,0:T(8,128)(2,1)}), bf16[4,64,32,128]{3,2,1,0:T(8,128)(2,1)}) %all-gather.7.cloned.1.call-update) | async-done | bytes 2097168 | tf_op jit(solution)/shard_map/all_gather | solution.py:13
  73.0 8.2 %while.29 = (s32[]{:T(128)}, f32[64,32,128]{2,1,0:T(8,128)S(1)}, s32[]{:T(128)}, bf16[4,64,32,128]{3,2,1,0:T(8,128)(2,1)}, bf16[4,64]{1,0:T(4,128)(2,1)}, /*index=5*/s32[]{:T(128)}, s32[]{:T(128)}) while((s32[]{:T(128)}, f32[64,32,128]{2,1,0:T(8,128)S(1)}, s32[]{:T(128)}, bf16[4,64,32,128]{3,2,1,0:T(8,128)(2,1)}, ...), condition=%wide.region_5.6_spmd.clone, body=%wide.region_4.5_spmd.clone.sunk | while | flops 1310788 | bytes 2622185 | solution.py:30
  73.7 1.4 fusion.60
  75.8 1.4 fusion.60
  77.8 1.4 fusion.60
  79.9 1.4 fusion.60
  81.3 5.4 %fusion.3 = (f32[128,4,16]{0,2,1:T(8,128)}, f32[128,4,128]{0,2,1:T(8,128)}) fusion(f32[128,4,128]{0,2,1:T(8,128)} %convert_element_type.107, f32[128,4,16]{0,2,1:T(8,128)} %copy-done.19, f32[4,16,32,128]{3,2,1,0:T(8,128)S(1)} %bitcast.110, bf16[128,4,16,32]{0,3,2,1:T(8,128)(2,1)} %bitcast.121), kind=kOutput, calls=%fused_computation.10 | convolution fusion | flops 406773760 | bytes 2162688 | tf_op jit(solution)/shard_map/tgkp,gkpn->tgkn/dot_general | solution.py:128
  86.6 67.5 %all-gather.5.cloned.1.call-done = f32[4,64,32,128]{3,2,1,0:T(8,128)} async-done(((f32[1,64,32,128]{3,2,1,0:T(8,128)}), f32[4,64,32,128]{3,2,1,0:T(8,128)}) %all-gather.5.cloned.1.call-update) | async-done | bytes 4194320 | tf_op jit(solution)/shard_map/all_gather | solution.py:35
  154.2 4.6 %rev.12 = f32[4,64,32,128]{3,2,1,0:T(8,128)} reverse(f32[4,64,32,128]{3,2,1,0:T(8,128)} %all-gather.5.cloned.1.call-done), dimensions={0} | reverse | bytes 8388608 | tf_op jit(solution)/shard_map/rev | solution.py:36
  158.8 6.6 %while.28 = (s32[]{:T(128)}, f32[64,32,128]{2,1,0:T(8,128)S(1)}, s32[]{:T(128)}, f32[4,64,32,128]{3,2,1,0:T(8,128)}, f32[4,64]{1,0:T(4,128)}, /*index=5*/s32[]{:T(128)}, s32[]{:T(128)}) while((s32[]{:T(128)}, f32[64,32,128]{2,1,0:T(8,128)S(1)}, s32[]{:T(128)}, f32[4,64,32,128]{3,2,1,0:T(8,128)}, f32[4,64]{1,0:T(4,128)}, ...), condition=%wide.region_2.3_spmd.clone, body=%wide.region_1.2_spmd.clone.sunk | while | flops 1048580 | bytes 3146601 | solution.py:46
  159.5 1.5 fusion.59
  161.6 1.5 fusion.59
  163.8 1.5 fusion.59
  165.4 1.1 multiply_reduce_fusion.2
  167.2 4.9 %fusion.23 = (f32[128,4,16]{0,2,1:T(8,128)S(1)}, f32[128,4,16]{0,2,1:T(8,128)}, bf16[128,4,16,32]{0,3,2,1:T(8,128)(2,1)}) fusion(f32[128,4,16,32]{0,3,2,1:T(8,128)S(1)} %convolution_bitcast_fusion.1, bf16[128,4,16,32]{0,3,2,1:T(8,128)(2,1)S(1)} %bitcast.113, f32[128,4,16]{0,2,1:T(8,128)S(1)} %bitcast.132, f32[128,4,16]{0,2,1:T(8,128)S(1)} %copy-done.23, ...), kind=kOutput, calls=%fused_computation.38 | convolution fusion | flops 409190400 | bytes 3063808 | tf_op jit(solution)/shard_map/gkts,tgkp->sgkp/dot_general | solution.py:115
  173.6 1.0 copy.88
  175.6 1.5 convolution_bitcast_fusion
  177.5 1.3 fusion.21
  179.6 1.8 fusion.18
  181.4 30.4 %reduce-scatter.2.cloned.1.call-done = f32[512,64]{0,1:T(8,128)} async-done(((f32[4096,64]{0,1:T(8,128)}), f32[512,64]{0,1:T(8,128)}) %reduce-scatter.2.cloned.1.call-update) | async-done | bytes 131088 | tf_op jit(solution)/shard_map/reduce_scatter | solution.py:139
  212.9 2.0 copy.90
  215.0 33.7 %all-reduce.2.cloned.1.call-done = f32[512,64]{0,1:T(8,128)} async-done(((f32[512,64]{0,1:T(8,128)}), f32[512,64]{0,1:T(8,128)}) %all-reduce.2.cloned.1.call-update) | async-done | bytes 131088 | tf_op jit(solution)/shard_map/psum | solution.py:142
  248.7 1.6 copy.131
  (103 shorter events, 16.8 us)
Async XLA Ops:
  7.2 12.5 %copy-start = (bf16[1,128,4096]{2,1,0:T(8,128)(2,1)S(1)}, bf16[1,128,4096]{2,1,0:T(8,128)(2,1)}, u32[]{:S(2)}) copy-start(bf16[1,128,4096]{2,1,0:T(8,128)(2,1)} %param.12) | copy-start | bytes 3145732
  7.2 19.8 %copy-start.12 = (bf16[1,128,2048]{2,1,0:T(8,128)(2,1)S(1)}, bf16[1,128,2048]{2,1,0:T(8,128)(2,1)}, u32[]{:S(2)}) copy-start(bf16[1,128,2048]{2,1,0:T(8,128)(2,1)} %param.19) | copy-start | bytes 1572868
  7.2 20.1 %copy-start.16 = (bf16[1,128,512]{2,1,0:T(8,128)(2,1)S(1)}, bf16[1,128,512]{2,1,0:T(8,128)(2,1)}, u32[]{:S(2)}) copy-start(bf16[1,128,512]{2,1,0:T(8,128)(2,1)} %param.18) | copy-start | bytes 393220
  7.2 65.8 %all-gather.7.cloned.1.call-start = ((), (), s32[]{:S(2)}) async-start(), calls=%async_computation.2 | async-start | bytes 2621440 | tf_op jit(solution)/shard_map/all_gather | solution.py:13
  21.4 5.5 %copy-start.17 = (f32[128,64]{0,1:T(8,128)}, f32[128,64]{0,1:T(8,128)S(1)}, u32[]{:S(2)}) copy-start(f32[128,64]{0,1:T(8,128)S(1)} %get-tuple-element.281) | copy-start | bytes 98308
  22.3 4.6 %copy-start.9 = (f32[128,64]{0,1:T(8,128)}, f32[128,64]{0,1:T(8,128)S(1)}, u32[]{:S(2)}) copy-start(f32[128,64]{0,1:T(8,128)S(1)} %copy.76) | copy-start | bytes 98308
  24.7 4.4 %copy-start.1 = (bf16[1,128,2048]{1,2,0:T(8,128)(2,1)}, bf16[1,128,2048]{1,2,0:T(8,128)(2,1)S(1)}, u32[]{:S(2)}) copy-start(bf16[1,128,2048]{1,2,0:T(8,128)(2,1)S(1)} %copy.82) | copy-start | bytes 1572868
  25.4 1.5 copy-start.7
  25.5 3.8 %copy-start.19 = (f32[128,4,16]{0,2,1:T(8,128)}, f32[128,4,16]{0,2,1:T(8,128)S(1)}, u32[]{:S(2)}) copy-start(f32[128,4,16]{0,2,1:T(8,128)S(1)} %get-tuple-element.280) | copy-start | bytes 98308
  26.9 127.2 %all-gather.5.cloned.1.call-start = ((), (), s32[]{:S(2)}) async-start(), calls=%async_computation.1 | async-start | bytes 5242880 | tf_op jit(solution)/shard_map/all_gather | solution.py:35
  27.3 1.8 copy-start.4
  29.0 182.9 %reduce-scatter.2.cloned.1.call-start = ((), (), s32[]{:S(2)}) async-start(), calls=%async_computation.3 | async-start | bytes 1179648 | tf_op jit(solution)/shard_map/reduce_scatter | solution.py:139
  52.1 0.6 copy-start.24
  52.3 0.7 copy-start.14
  165.3 1.8 copy-start.2
  165.3 1.8 copy-start.5
  165.4 1.8 copy-start.10
  165.4 1.8 copy-start.15
  165.4 1.8 copy-start.18
  165.4 1.8 copy-start.23
  165.4 1.8 copy-start.25
  167.2 5.0 %copy-start.13 = (f32[128,64]{0,1:T(8,128)S(1)}, f32[128,64]{0,1:T(8,128)}, u32[]{:S(2)}) copy-start(f32[128,64]{0,1:T(8,128)} %get-tuple-element.283) | copy-start | bytes 98308
  167.2 5.2 %copy-start.26 = (f32[64]{0:T(128)S(1)}, f32[64]{0:T(128)}, u32[]{:S(2)}) copy-start(f32[64]{0:T(128)} %multiply_reduce_fusion.2) | copy-start | bytes 772
  167.2 5.3 %copy-start.8 = (f32[128,4,16]{0,2,1:T(8,128)S(1)}, f32[128,4,16]{0,2,1:T(8,128)}, u32[]{:S(2)}) copy-start(f32[128,4,16]{0,2,1:T(8,128)} %copy-done.7) | copy-start | bytes 98308
  167.2 5.3 %copy-start.11 = (f32[128,64]{0,1:T(8,128)S(1)}, f32[128,64]{0,1:T(8,128)}, u32[]{:S(2)}) copy-start(f32[128,64]{0,1:T(8,128)} %copy-done.9) | copy-start | bytes 98308
  167.2 5.3 %copy-start.20 = (f32[4,16,128]{2,1,0:T(8,128)S(1)}, f32[4,16,128]{2,1,0:T(8,128)}, u32[]{:S(2)}) copy-start(f32[4,16,128]{2,1,0:T(8,128)} %get-tuple-element.246) | copy-start | bytes 98308
  167.2 5.3 %copy-start.21 = (f32[4,16,128]{2,1,0:T(8,128)S(1)}, f32[4,16,128]{2,1,0:T(8,128)}, u32[]{:S(2)}) copy-start(f32[4,16,128]{2,1,0:T(8,128)} %get-tuple-element.247) | copy-start | bytes 98308
  167.2 5.3 %copy-start.22 = (f32[128,4,16]{0,2,1:T(8,128)S(1)}, f32[128,4,16]{0,2,1:T(8,128)}, u32[]{:S(2)}) copy-start(f32[128,4,16]{0,2,1:T(8,128)} %get-tuple-element.249) | copy-start | bytes 98308
  172.1 5.4 %copy-start.6 = (f32[4,128,128]{2,1,0:T(8,128)S(1)}, f32[4,128,128]{2,1,0:T(8,128)}, u32[]{:S(2)}) copy-start(f32[4,128,128]{2,1,0:T(8,128)} %get-tuple-element.248) | copy-start | bytes 786436
  172.1 7.5 %copy-start.3 = (bf16[1,128,2048]{1,2,0:T(8,128)(2,1)S(1)}, bf16[1,128,2048]{1,2,0:T(8,128)(2,1)}, u32[]{:S(2)}) copy-start(bf16[1,128,2048]{1,2,0:T(8,128)(2,1)} %copy-done.1) | copy-start | bytes 1572868
  177.2 71.5 %all-reduce.2.cloned.1.call-start = ((), (), s32[]{:S(2)}) async-start(), calls=%async_computation.4 | async-start | bytes 262144 | tf_op jit(solution)/shard_map/psum | solution.py:142
Sparse Core Ops, SparseCore 0:
  27.0 45.9 all-gather.6
  74.6 79.5 all-gather.4
  177.3 34.4 reduce-scatter.1
  214.0 34.6 all-reduce.1
where the time goes:
time: 258 us; the launch traced here: 257 us
  waiting for transfers between devices  147 us (57%)
  blocking collectives  31.8 us (12%)
  matrix products  26 us (10%)
  local copies, waits for them, and re-layouts  19.2 us (7%)
  other arithmetic  18.5 us (7%)
  between operations  14.3 us (6%)
    all_gather x1, waiting for transfers between devices, prefix(): pieces = jax.tree.map(lambda part: lax.all_gather(part, axis), value)  67.5 us
    psum x1, waiting for transfers between devices, body(): grad_weight = lax.psum(partial_rows, 'seq')  33.7 us
    reduce_scatter x1, waiting for transfers between devices, body(): lax.psum_scatter(jnp.dot(columns.T, grad_raw, precision=HIGH), 'fsdp', sc...  30.4 us
    all_gather x1, waiting for transfers between devices, entering(): lax.all_gather(part.astype(kind), axis)  14.8 us
    all_gather x1, blocking collectives, body(): lax.all_gather(dt_weight, 'fsdp', axis=0, tiled=True)  11.8 us
    all_gather x1, blocking collectives, prefix(): pieces = jax.tree.map(lambda part: lax.all_gather(part, axis), value)  11.6 us
    all_gather x1, blocking collectives, entering(): lax.all_gather(part.astype(kind), axis)  8.39 us
    unnamed x61, local copies, waits for them, and re-layouts  8.16 us
  transfers between devices with their start and end apart: 4, of which 4 were waited for; matrix products, arithmetic and copies ran while one was open for 12% of the time, Pallas kernels for 0%

commit v1 on v0

--- a/solution.py
+++ b/solution.py
@@ -139,7 +139,7 @@
     partial_rows = lax.psum_scatter(
         jnp.dot(columns.T, grad_raw, precision=HIGH), "fsdp", scatter_dimension=0, tiled=True
     )
-    grad_weight = lax.psum(partial_rows, "seq")
+    grad_weight = jax.lax.all_gather(partial_rows, "seq").sum(axis=0)
     out_x = grad_x.reshape(1, length, heads * head_size).astype(jnp.bfloat16)
     out_b = grad_b.reshape(1, length, groups * STATE).astype(jnp.bfloat16)
     out_c = grad_c.reshape(1, length, groups * STATE).astype(jnp.bfloat16)

time: 258 us -> 238 us (0.922)
  waiting for transfers between devices: 147 us -> 111 us
  blocking collectives: 31.8 us -> 46.9 us
    psum x1 -> x0, waiting for transfers between devices: 33.7 us -> none  [body(): grad_weight = lax.psum(partial_rows, 'seq')]
    all_gather x0 -> x1, blocking collectives: none -> 15.6 us  [body(): grad_weight = jax.lax.all_gather(partial_rows, 'seq').sum(axis=0)]
    reduce_scatter x1, waiting for transfers between devices: 30.4 us -> 27.6 us  [body(): lax.psum_scatter(jnp.dot(columns.T, grad_raw, precision=HIGH), 'fsdp', sc...]
    unnamed x61 -> x52, local copies, waits for them, and re-layouts: 8.16 us -> 6.55 us
  transfers between devices with their start and end apart: 4 -> 3, of which waited for: 4 -> 3; matrix products, arithmetic and copies ran while one was open for 12% -> 13% of each run, Pallas kernels for 0% -> 0%
where the time goes in v1:
time: 238 us; the launch traced here: 237 us
  waiting for transfers between devices  111 us (47%)
  blocking collectives  46.9 us (20%)
  matrix products  26.1 us (11%)
  other arithmetic  20.2 us (8%)
  local copies, waits for them, and re-layouts  18.6 us (8%)
  between operations  14.2 us (6%)
    all_gather x1, waiting for transfers between devices, prefix(): pieces = jax.tree.map(lambda part: lax.all_gather(part, axis), value)  67.7 us
    reduce_scatter x1, waiting for transfers between devices, body(): lax.psum_scatter(jnp.dot(columns.T, grad_raw, precision=HIGH), 'fsdp', sc...  27.6 us
    all_gather x1, blocking collectives, body(): grad_weight = jax.lax.all_gather(partial_rows, 'seq').sum(axis=0)  15.6 us
    all_gather x1, waiting for transfers between devices, entering(): lax.all_gather(part.astype(kind), axis)  15.4 us
    all_gather x1, blocking collectives, body(): lax.all_gather(dt_weight, 'fsdp', axis=0, tiled=True)  11.8 us
    all_gather x1, blocking collectives, prefix(): pieces = jax.tree.map(lambda part: lax.all_gather(part, axis), value)  11.4 us
    all_gather x1, blocking collectives, entering(): lax.all_gather(part.astype(kind), axis)  8.06 us
    unnamed x52, local copies, waits for them, and re-layouts  6.55 us
  transfers between devices with their start and end apart: 3, of which 3 were waited for; matrix products, arithmetic and copies ran while one was open for 13% of the time, Pallas kernels for 0%

profile of v1, /device:TPU:0, one launch (start us, length us, event | category | flops | bytes accessed | tf_op | source)
XLA Modules:
  0.0 236.8 jit_solution(5984092048151173802)
XLA Ops:
  7.2 11.8 %all_gather.23 = bf16[4096,64]{0,1:T(8,128)(2,1)S(1)} all-gather(bf16[512,64]{0,1:T(8,128)(2,1)} %param.13), channel_id=1, replica_groups=mesh['fsdp'=8,'seq'=4] {'fsdp'}, dimensions={0}, use_global_device_ids=true | all-gather | bytes 589824 | tf_op jit(solution)/shard_map/all_gather | solution.py:68
  19.7 1.8 compare_select_fusion
  22.5 0.9 reshape_squeeze.13
  23.4 1.3 copy.82
  25.5 1.4 convolution_convert_fusion
  27.4 1.7 fusion.26
  30.2 11.4 %all-gather.1 = f32[4,1,64]{2,1,0:T(1,128)S(1)} all-gather(f32[1,1,64]{2,1,0:T(1,128)} %get-tuple-element.277), channel_id=1, replica_groups=mesh['fsdp'=8,'seq'=4] {'seq'}, dimensions={0}, use_global_device_ids=true | all-gather | bytes 1280 | tf_op jit(solution)/shard_map/all_gather | solution.py:35
  42.3 8.1 %all-gather.2 = bf16[4,1,64]{2,1,0:T(2,128)(2,1)S(1)} all-gather(bf16[1,1,64]{2,1,0:T(2,128)(2,1)} %get-tuple-element.278), channel_id=1, replica_groups=mesh['fsdp'=8,'seq'=4] {'seq'}, dimensions={0}, use_global_device_ids=true | all-gather | bytes 640 | tf_op jit(solution)/shard_map/all_gather | solution.py:13
  52.6 5.1 %multiply_reduce_fusion = (f32[4,16,128]{2,1,0:T(8,128)}, f32[4,16,128]{2,1,0:T(8,128)}, f32[4,128,128]{2,1,0:T(8,128)}) fusion(f32[4,128,128]{2,1,0:T(8,128)S(1)} %fusion.40, f32[4,16,128]{2,1,0:T(8,128)} %bitcast.133, bf16[128,4,16,32]{0,3,2,1:T(8,128)(2,1)} %bitcast.122, bf16[128,4,16,32]{0,3,2,1:T(8,128)(2,1)} %bitcast.114, ...), kind=kOutput, calls=%fused_computation.15 | convolution fusion | flops 76464128 | bytes 1720320 | tf_op jit(solution)/shard_map/tgkp,sgkp->gkts/dot_general | solution.py:112
  57.7 15.4 %all-gather.8.cloned.1.call-done = bf16[4,64,32,128]{3,2,1,0:T(8,128)(2,1)} async-done(((bf16[1,64,32,128]{3,2,1,0:T(8,128)(2,1)}), bf16[4,64,32,128]{3,2,1,0:T(8,128)(2,1)}) %all-gather.8.cloned.1.call-update) | async-done | bytes 2097168 | tf_op jit(solution)/shard_map/all_gather | solution.py:13
  73.1 8.0 %while.29 = (s32[]{:T(128)}, f32[64,32,128]{2,1,0:T(8,128)S(1)}, s32[]{:T(128)}, bf16[4,64,32,128]{3,2,1,0:T(8,128)(2,1)}, bf16[4,64]{1,0:T(4,128)(2,1)}, /*index=5*/s32[]{:T(128)}, s32[]{:T(128)}) while((s32[]{:T(128)}, f32[64,32,128]{2,1,0:T(8,128)S(1)}, s32[]{:T(128)}, bf16[4,64,32,128]{3,2,1,0:T(8,128)(2,1)}, ...), condition=%wide.region_5.6_spmd.clone, body=%wide.region_4.5_spmd.clone.sunk | while | flops 1310788 | bytes 2622185 | solution.py:30
  73.7 1.4 fusion.60
  75.7 1.4 fusion.60
  77.7 1.4 fusion.60
  79.7 1.4 fusion.60
  81.2 5.4 %fusion.3 = (f32[128,4,16]{0,2,1:T(8,128)}, f32[128,4,128]{0,2,1:T(8,128)}) fusion(f32[128,4,128]{0,2,1:T(8,128)} %convert_element_type.107, f32[128,4,16]{0,2,1:T(8,128)} %copy-done.19, f32[4,16,32,128]{3,2,1,0:T(8,128)S(1)} %bitcast.112, bf16[128,4,16,32]{0,3,2,1:T(8,128)(2,1)} %bitcast.123), kind=kOutput, calls=%fused_computation.10 | convolution fusion | flops 406773760 | bytes 2162688 | tf_op jit(solution)/shard_map/tgkp,gkpn->tgkn/dot_general | solution.py:128
  86.6 67.7 %all-gather.6.cloned.1.call-done = f32[4,64,32,128]{3,2,1,0:T(8,128)} async-done(((f32[1,64,32,128]{3,2,1,0:T(8,128)}), f32[4,64,32,128]{3,2,1,0:T(8,128)}) %all-gather.6.cloned.1.call-update) | async-done | bytes 4194320 | tf_op jit(solution)/shard_map/all_gather | solution.py:35
  154.3 4.6 %rev.12 = f32[4,64,32,128]{3,2,1,0:T(8,128)} reverse(f32[4,64,32,128]{3,2,1,0:T(8,128)} %all-gather.6.cloned.1.call-done), dimensions={0} | reverse | bytes 8388608 | tf_op jit(solution)/shard_map/rev | solution.py:36
  158.8 6.5 %while.28 = (s32[]{:T(128)}, f32[64,32,128]{2,1,0:T(8,128)S(1)}, s32[]{:T(128)}, f32[4,64,32,128]{3,2,1,0:T(8,128)}, f32[4,64]{1,0:T(4,128)}, /*index=5*/s32[]{:T(128)}, s32[]{:T(128)}) while((s32[]{:T(128)}, f32[64,32,128]{2,1,0:T(8,128)S(1)}, s32[]{:T(128)}, f32[4,64,32,128]{3,2,1,0:T(8,128)}, f32[4,64]{1,0:T(4,128)}, ...), condition=%wide.region_2.3_spmd.clone, body=%wide.region_1.2_spmd.clone.sunk | while | flops 1048580 | bytes 3146601 | solution.py:46
  159.5 1.5 fusion.59
  161.7 1.5 fusion.59
  163.9 1.5 fusion.59
  165.5 1.1 multiply_reduce_fusion.2
  167.3 4.9 %fusion.23 = (f32[128,4,16]{0,2,1:T(8,128)S(1)}, f32[128,4,16]{0,2,1:T(8,128)}, bf16[128,4,16,32]{0,3,2,1:T(8,128)(2,1)}) fusion(f32[128,4,16,32]{0,3,2,1:T(8,128)S(1)} %convolution_bitcast_fusion.1, bf16[128,4,16,32]{0,3,2,1:T(8,128)(2,1)S(1)} %bitcast.115, f32[128,4,16]{0,2,1:T(8,128)S(1)} %bitcast.134, f32[128,4,16]{0,2,1:T(8,128)S(1)} %copy-done.20, ...), kind=kOutput, calls=%fused_computation.38 | convolution fusion | flops 409190400 | bytes 3063808 | tf_op jit(solution)/shard_map/gkts,tgkp->sgkp/dot_general | solution.py:115
  175.2 1.0 copy.88
  177.2 1.6 convolution_bitcast_fusion
  178.8 1.3 fusion.21
  180.9 1.8 fusion.18
  183.8 2.1 copy.90
  185.8 27.6 %reduce-scatter.2.cloned.1.call-done = f32[512,64]{0,1:T(8,128)} async-done(((f32[4096,64]{0,1:T(8,128)}), f32[512,64]{0,1:T(8,128)}) %reduce-scatter.2.cloned.1.call-update) | async-done | bytes 131088 | tf_op jit(solution)/shard_map/reduce_scatter | solution.py:139
  213.4 15.6 %all-gather = f32[2048,64]{0,1:T(8,128)S(1)} all-gather(f32[512,64]{0,1:T(8,128)} %reduce-scatter.2.cloned.1.call-done), channel_id=2, replica_groups=mesh['fsdp'=8,'seq'=4] {'seq'}, dimensions={0}, use_global_device_ids=true | all-gather | bytes 655360 | tf_op jit(solution)/shard_map/all_gather | solution.py:142
  229.3 1.0 reduce_sum.98
  (94 shorter events, 18.1 us)
Async XLA Ops:
  7.2 12.5 %copy-start = (bf16[1,128,4096]{2,1,0:T(8,128)(2,1)S(1)}, bf16[1,128,4096]{2,1,0:T(8,128)(2,1)}, u32[]{:S(2)}) copy-start(bf16[1,128,4096]{2,1,0:T(8,128)(2,1)} %param.12) | copy-start | bytes 3145732
  7.2 19.9 %copy-start.12 = (bf16[1,128,2048]{2,1,0:T(8,128)(2,1)S(1)}, bf16[1,128,2048]{2,1,0:T(8,128)(2,1)}, u32[]{:S(2)}) copy-start(bf16[1,128,2048]{2,1,0:T(8,128)(2,1)} %param.19) | copy-start | bytes 1572868
  7.2 20.2 %copy-start.16 = (bf16[1,128,512]{2,1,0:T(8,128)(2,1)S(1)}, bf16[1,128,512]{2,1,0:T(8,128)(2,1)}, u32[]{:S(2)}) copy-start(bf16[1,128,512]{2,1,0:T(8,128)(2,1)} %param.18) | copy-start | bytes 393220
  7.2 65.9 %all-gather.8.cloned.1.call-start = ((), (), s32[]{:S(2)}) async-start(), calls=%async_computation.2 | async-start | bytes 2621440 | tf_op jit(solution)/shard_map/all_gather | solution.py:13
  21.4 5.6 %copy-start.17 = (f32[128,64]{0,1:T(8,128)}, f32[128,64]{0,1:T(8,128)S(1)}, u32[]{:S(2)}) copy-start(f32[128,64]{0,1:T(8,128)S(1)} %get-tuple-element.281) | copy-start | bytes 98308
  22.4 4.6 %copy-start.9 = (f32[128,64]{0,1:T(8,128)}, f32[128,64]{0,1:T(8,128)S(1)}, u32[]{:S(2)}) copy-start(f32[128,64]{0,1:T(8,128)S(1)} %copy.76) | copy-start | bytes 98308
  24.7 4.4 %copy-start.1 = (bf16[1,128,2048]{1,2,0:T(8,128)(2,1)}, bf16[1,128,2048]{1,2,0:T(8,128)(2,1)S(1)}, u32[]{:S(2)}) copy-start(bf16[1,128,2048]{1,2,0:T(8,128)(2,1)S(1)} %copy.82) | copy-start | bytes 1572868
  25.5 1.5 copy-start.7
  25.5 3.8 %copy-start.19 = (f32[128,4,16]{0,2,1:T(8,128)}, f32[128,4,16]{0,2,1:T(8,128)S(1)}, u32[]{:S(2)}) copy-start(f32[128,4,16]{0,2,1:T(8,128)S(1)} %get-tuple-element.280) | copy-start | bytes 98308
  27.0 127.2 %all-gather.6.cloned.1.call-start = ((), (), s32[]{:S(2)}) async-start(), calls=%async_computation.1 | async-start | bytes 5242880 | tf_op jit(solution)/shard_map/all_gather | solution.py:35
  27.4 1.8 copy-start.4
  29.1 184.3 %reduce-scatter.2.cloned.1.call-start = ((), (), s32[]{:S(2)}) async-start(), calls=%async_computation.3 | async-start | bytes 1179648 | tf_op jit(solution)/shard_map/reduce_scatter | solution.py:139
  51.6 0.6 copy-start.21
  51.9 0.7 copy-start.14
  165.4 1.8 copy-start.2
  165.4 1.8 copy-start.5
  165.4 1.8 copy-start.10
  165.4 1.8 copy-start.15
  165.4 1.8 copy-start.18
  165.4 1.8 copy-start.20
  165.5 1.8 copy-start.22
  167.3 4.9 %copy-start.13 = (f32[128,64]{0,1:T(8,128)S(1)}, f32[128,64]{0,1:T(8,128)}, u32[]{:S(2)}) copy-start(f32[128,64]{0,1:T(8,128)} %get-tuple-element.283) | copy-start | bytes 98308
  167.3 5.9 %copy-start.8 = (f32[128,4,16]{0,2,1:T(8,128)S(1)}, f32[128,4,16]{0,2,1:T(8,128)}, u32[]{:S(2)}) copy-start(f32[128,4,16]{0,2,1:T(8,128)} %copy-done.7) | copy-start | bytes 98308
  167.3 5.9 %copy-start.11 = (f32[128,64]{0,1:T(8,128)S(1)}, f32[128,64]{0,1:T(8,128)}, u32[]{:S(2)}) copy-start(f32[128,64]{0,1:T(8,128)} %copy-done.9) | copy-start | bytes 98308
  172.2 6.6 %copy-start.6 = (f32[4,128,128]{2,1,0:T(8,128)S(1)}, f32[4,128,128]{2,1,0:T(8,128)}, u32[]{:S(2)}) copy-start(f32[4,128,128]{2,1,0:T(8,128)} %get-tuple-element.248) | copy-start | bytes 786436
  172.2 8.7 %copy-start.3 = (bf16[1,128,2048]{1,2,0:T(8,128)(2,1)S(1)}, bf16[1,128,2048]{1,2,0:T(8,128)(2,1)}, u32[]{:S(2)}) copy-start(bf16[1,128,2048]{1,2,0:T(8,128)(2,1)} %copy-done.1) | copy-start | bytes 1572868
Sparse Core Ops, SparseCore 0:
  27.1 45.9 all-gather.7
  74.7 79.5 all-gather.5
  178.9 34.4 reduce-scatter.1
